TPU v7x, 256 devices: a whole 4x4x8 slice. The times are simulated.
256 devices in a mesh: seq: 64 (over x, z, core), grp: 4 (over y).
Axes of the slice: x: 4, y: 4, z: 8, core: 2. Of those that a mesh axis runs over, the one named last changes fastest.
Arguments:
- delta_codes: int32 [16, 16, 16384, 128], P('grp', None, 'seq'), may hold values from -63 to 63, as said below
- scale_index: int32 [16, 16, 1024], P('grp', None, 'seq'), may hold values from 0 to 15
- anchor_codes: int32 [16, 16, 128], P('grp'), may hold values from -8 to 7
- scale_table: float32 [16, 128], replicated, may hold values from 5e-05 to 0.0005
- anchor_scale: float32 [128], replicated, may hold values from 0.0001 to 0.001
Outputs:
- decode_cache: bfloat16 [4, 64, 16384, 128], P('grp', 'seq')
Inputs may be any that keep to these rules, and one draw needn't show every extreme that they name: `delta_codes`: for every sequence, head and channel, the running sum of the codes from the sequence's first token lies in -32 .. 31 after every token, and in -2 .. 1 after the last token of each group of 16 tokens.
All inputs are finite; a program needn't handle non-finite values.
Results may differ from a plain program's by a relative error of at most 0.001.
Values may be sent and summed in bfloat16 or wider, within the bound.
A program may use at most 128 MiB of HBM per device.

v0:
```python
import jax
import jax.numpy as jnp
from jax import lax
from jax.sharding import PartitionSpec as P


def lookup_scales(scale_ids, scale_table):
    levels = scale_table.shape[0]
    onehot = (scale_ids[..., None] == jnp.arange(levels, dtype=jnp.int32)).astype(jnp.float32)
    flat = jnp.dot(
        onehot.reshape(-1, levels),
        scale_table,
        precision=lax.Precision.HIGHEST,
        preferred_element_type=jnp.float32,
    )
    return flat.reshape(scale_ids.shape + (scale_table.shape[1],))


def dequantize(code_vals, scale_ids, scale_table):
    head_dim = code_vals.shape[-1]
    steps_len = code_vals.shape[-2]
    groups = scale_ids.shape[-1]
    scales = lookup_scales(scale_ids, scale_table)
    lead_dims = code_vals.shape[:-2]
    shaped = code_vals.astype(jnp.float32).reshape(
        lead_dims + (groups, steps_len // groups, head_dim)
    )
    return (shaped * scales[..., :, None, :]).reshape(code_vals.shape)


def block_prefix(deltas):
    tok_len = deltas.shape[1]
    lower_ones = (jnp.arange(tok_len)[:, None] >= jnp.arange(tok_len)[None, :]).astype(jnp.float32)
    return jnp.einsum("tu,ruc->rtc", lower_ones, deltas, precision=lax.Precision.HIGHEST)


def finish_rows(prefix_rows, totals, seq_count):
    strict = (jnp.arange(seq_count)[:, None] > jnp.arange(seq_count)[None, :]).astype(jnp.float32)
    carried = jnp.einsum("ij,rjc->ric", strict, totals, precision=lax.Precision.HIGHEST)
    row_count, length, head_dim = prefix_rows.shape
    shaped = (
        prefix_rows.reshape(row_count, seq_count, length // seq_count, head_dim)
        + carried[:, :, None, :]
    )
    return shaped.astype(jnp.bfloat16).reshape(row_count, length, head_dim)


def on_device(delta_codes, scale_index, anchor_codes, scale_table, anchor_scale):
    seq_count = lax.axis_size("seq")
    seq_local, kv_heads, tok_dev, head_dim = delta_codes.shape
    packed = (
        delta_codes.astype(jnp.bfloat16),
        scale_index.astype(jnp.bfloat16),
        anchor_codes.astype(jnp.bfloat16),
    )
    sectioned = (
        lax.all_to_all(packed[0], "grp", split_axis=1, concat_axis=0, tiled=True),
        lax.all_to_all(packed[1], "grp", split_axis=1, concat_axis=0, tiled=True),
        lax.all_to_all(packed[2], "grp", split_axis=1, concat_axis=0, tiled=True),
    )
    code_rows = sectioned[0].reshape(-1, tok_dev, head_dim)
    id_rows = sectioned[1].reshape(code_rows.shape[0], -1)
    anchor_rows = sectioned[2].reshape(code_rows.shape[0], head_dim)
    moved = (
        lax.all_to_all(code_rows, "seq", split_axis=0, concat_axis=1, tiled=True),
        lax.all_to_all(id_rows, "seq", split_axis=0, concat_axis=1, tiled=True),
    )
    row_count = moved[0].shape[0]
    start = lax.axis_index("seq") * row_count
    my_anchor = lax.dynamic_slice_in_dim(anchor_rows, start, row_count, 0)
    anchor_vals = my_anchor.astype(jnp.float32) * anchor_scale
    deltas = dequantize(moved[0], moved[1].astype(jnp.int32), scale_table)
    prefix = block_prefix(deltas.reshape(-1, tok_dev, head_dim)).reshape(
        row_count, seq_count, tok_dev, head_dim
    )
    totals = prefix[:, :, -1, :]
    prefix_rows = (prefix + anchor_vals[:, None, None, :]).reshape(row_count, -1, head_dim)
    result = finish_rows(prefix_rows, totals, seq_count)
    return result[None]


def solution(mesh):
    placed = (P("grp", None, "seq", None), P("grp", None, "seq"), P("grp", None, None), P(), P())
    return jax.shard_map(
        on_device,
        mesh=mesh,
        in_specs=placed,
        out_specs=P("grp", "seq", None, None),
        check_vma=False,
    )
```

profile of v0, /device:TPU:3, one launch (start us, length us, event | category | flops | bytes accessed | tf_op | source)
XLA Modules:
  0.0 227.0 jit_solution(3346207164019680870)
XLA Ops:
  0.0 0.0 copy-start
  0.0 0.8 fusion.8
  0.8 0.1 reshape.92
  0.9 8.1 %all_to_all.67 = bf16[4,2,128]{2,1,0:T(2,128)(2,1)S(1)} all-to-all(bf16[4,2,128]{2,1,0:T(2,128)(2,1)S(1)} %reshape.92), channel_id=1, replica_groups=mesh['seq'=64,'grp'=4] {'grp'}, dimensions={0} | all-to-all | bytes 4096 | tf_op jit(solution)/shard_map/all_to_all | solution.py:58
  9.0 0.1 reshape.93
  9.1 0.6 copy.17
  9.7 13.7 %all-to-all-start.3 = ((bf16[64,1,16]{2,1,0:T(2,128)(2,1)}), bf16[64,1,16]{2,1,0:T(2,128)(2,1)S(1)}, u32[]{:S(2)}, u32[]{:S(2)}) async-start(bf16[64,1,16]{2,1,0:T(2,128)(2,1)} %copy.17), calls=%async_computation.3 | async-start | bytes 65536 | tf_op jit(solution)/shard_map/all_to_all | solution.py:66
  23.5 0.0 copy-start.1
  23.5 6.4 %copy_convert_fusion = bf16[4,16,256,128]{3,2,0,1:T(8,128)(2,1)} fusion(s32[4,16,256,128]{3,2,1,0:T(8,128)} %param.5), kind=kLoop, calls=%fused_computation.4 | loop fusion | flops 2097152 | bytes 12582912 | tf_op jit(solution)/shard_map/convert_element_type | solution.py:52
  29.9 2.0 all-to-all-done.3
  31.8 4.8 %all-to-all-start = ((bf16[4,16,256,128]{3,2,0,1:T(8,128)(2,1)}), bf16[4,16,256,128]{3,2,0,1:T(8,128)(2,1)}, u32[]{:S(2)}, u32[]{:S(2)}) async-start(bf16[4,16,256,128]{3,2,0,1:T(8,128)(2,1)} %copy_convert_fusion), calls=%async_computation | async-start | bytes 8388608 | tf_op jit(solution)/shard_map/all_to_all | solution.py:57
  36.7 0.0 copy-done.1
  36.7 0.6 copy_convert_fusion.1
  37.3 47.7 %all-to-all-done = bf16[4,16,256,128]{3,2,0,1:T(8,128)(2,1)} async-done(((bf16[4,16,256,128]{3,2,0,1:T(8,128)(2,1)}), bf16[4,16,256,128]{3,2,0,1:T(8,128)(2,1)}, u32[]{:S(2)}, u32[]{:S(2)}) %all-to-all-start) | async-done | bytes 4194336 | tf_op jit(solution)/shard_map/all_to_all | solution.py:57
  85.0 3.2 %all-to-all-start.4 = ((bf16[4,16,128]{2,0,1:T(4,128)(2,1)}), bf16[4,16,128]{2,0,1:T(4,128)(2,1)S(1)}, u32[]{:S(2)}, u32[]{:S(2)}) async-start(bf16[4,16,128]{2,0,1:T(4,128)(2,1)} %copy_convert_fusion.1), calls=%async_computation.4 | async-start | bytes 32768 | tf_op jit(solution)/shard_map/all_to_all | solution.py:59
  88.2 0.0 copy-start.2
  88.2 4.7 %copy.14 = bf16[4,4,4,256,128]{4,3,2,0,1:T(8,128)(2,1)} copy(bf16[4,4,4,256,128]{4,3,0,2,1:T(8,128)(2,1)} %bitcast) | data formatting | bytes 8388608 | tf_op jit(solution)/shard_map/all_to_all | solution.py:57
  93.0 0.0 all-to-all-done.4
  93.0 10.3 %all-to-all-start.1 = ((bf16[64,256,128]{2,1,0:T(8,128)(2,1)}), bf16[64,256,128]{2,1,0:T(8,128)(2,1)}, u32[]{:S(2)}, u32[]{:S(2)}) async-start(bf16[64,256,128]{2,1,0:T(8,128)(2,1)} %bitcast.47), calls=%async_computation.1 | async-start | bytes 8388608 | tf_op jit(solution)/shard_map/all_to_all | solution.py:65
  103.2 0.1 convert_reduce_fusion
  103.4 0.1 reshape.82
  103.4 0.0 copy-done
  103.4 0.5 fusion.2
  103.9 0.0 copy-done.2
  104.0 95.0 %all-to-all-done.1 = bf16[64,256,128]{2,1,0:T(8,128)(2,1)} async-done(((bf16[64,256,128]{2,1,0:T(8,128)(2,1)}), bf16[64,256,128]{2,1,0:T(8,128)(2,1)}, u32[]{:S(2)}, u32[]{:S(2)}) %all-to-all-start.1) | async-done | bytes 4194336 | tf_op jit(solution)/shard_map/all_to_all | solution.py:65
  199.0 0.5 mul.16
  199.5 6.7 %bitcast_multiply_fusion = f32[64,256,128]{2,1,0:T(8,128)} fusion(bf16[64,256,128]{2,1,0:T(8,128)(2,1)} %all-to-all-done.1, f32[64,256,128]{2,1,0:T(8,128)S(1)} %bitcast.46), kind=kLoop, calls=%fused_computation.3 | loop fusion | flops 4194304 | bytes 20971520 | tf_op jit(solution)/shard_map/mul | solution.py:28
  206.2 9.4 %fusion.5 = f32[64,128,256]{2,1,0:T(8,128)S(1)} fusion(f32[64,256,128]{2,1,0:T(8,128)} %bitcast_multiply_fusion), kind=kOutput, calls=%fused_computation.12 | convolution fusion | flops 6442516480 | bytes 16777216 | tf_op jit(solution)/shard_map/tu,ruc->rtc/dot_general | solution.py:34
  215.6 2.2 slice_reduce_fusion
  217.9 0.1 convolution_bitcast_fusion
  218.0 2.6 %fusion.1 = bf16[64,256,128]{1,2,0:T(8,128)(2,1)} fusion(f32[64,128,256]{2,1,0:T(8,128)S(1)} %fusion.5, f32[64,128]{1,0:T(8,128)S(1)} %convolution_bitcast_fusion, f32[128]{0:T(128)S(1)} %fusion.7), kind=kLoop, calls=%fused_computation.2 | loop fusion | flops 6291456 | bytes 12616192 | tf_op jit(solution)/shard_map/convert_element_type | solution.py:45
  220.7 6.4 %copy.21 = bf16[64,256,128]{2,1,0:T(8,128)(2,1)} copy(bf16[64,256,128]{1,2,0:T(8,128)(2,1)} %fusion.1) | data formatting | bytes 8388608 | tf_op jit(solution)/shard_map/convert_element_type | solution.py:45
  (3 shorter events, 0.0 us)
Async XLA Ops:
  0.0 103.4 %copy-start = (f32[16,128]{1,0:T(8,128)S(1)}, f32[16,128]{1,0:T(8,128)}, u32[]{:S(2)}) copy-start(f32[16,128]{1,0:T(8,128)} %param.8) | copy-start | bytes 24580
  9.7 22.1 %all-to-all-start.3 = ((bf16[64,1,16]{2,1,0:T(2,128)(2,1)}), bf16[64,1,16]{2,1,0:T(2,128)(2,1)S(1)}, u32[]{:S(2)}, u32[]{:S(2)}) async-start(bf16[64,1,16]{2,1,0:T(2,128)(2,1)} %copy.17), calls=%async_computation.3 | async-start | bytes 65536 | tf_op jit(solution)/shard_map/all_to_all | solution.py:66
  23.5 13.2 %copy-start.1 = (s32[4,16,128]{2,1,0:T(8,128)S(1)}, s32[4,16,128]{2,1,0:T(8,128)}, u32[]{:S(2)}) copy-start(s32[4,16,128]{2,1,0:T(8,128)} %param.7) | copy-start | bytes 98308
  31.8 53.2 %all-to-all-start = ((bf16[4,16,256,128]{3,2,0,1:T(8,128)(2,1)}), bf16[4,16,256,128]{3,2,0,1:T(8,128)(2,1)}, u32[]{:S(2)}, u32[]{:S(2)}) async-start(bf16[4,16,256,128]{3,2,0,1:T(8,128)(2,1)} %copy_convert_fusion), calls=%async_computation | async-start | bytes 8388608 | tf_op jit(solution)/shard_map/all_to_all | solution.py:57
  85.0 8.0 %all-to-all-start.4 = ((bf16[4,16,128]{2,0,1:T(4,128)(2,1)}), bf16[4,16,128]{2,0,1:T(4,128)(2,1)S(1)}, u32[]{:S(2)}, u32[]{:S(2)}) async-start(bf16[4,16,128]{2,0,1:T(4,128)(2,1)} %copy_convert_fusion.1), calls=%async_computation.4 | async-start | bytes 32768 | tf_op jit(solution)/shard_map/all_to_all | solution.py:59
  88.2 15.7 %copy-start.2 = (f32[128]{0:T(128)S(1)}, f32[128]{0:T(128)}, u32[]{:S(2)}) copy-start(f32[128]{0:T(128)} %param.9) | copy-start | bytes 1540
  93.0 106.0 %all-to-all-start.1 = ((bf16[64,256,128]{2,1,0:T(8,128)(2,1)}), bf16[64,256,128]{2,1,0:T(8,128)(2,1)}, u32[]{:S(2)}, u32[]{:S(2)}) async-start(bf16[64,256,128]{2,1,0:T(8,128)(2,1)} %bitcast.47), calls=%async_computation.1 | async-start | bytes 8388608 | tf_op jit(solution)/shard_map/all_to_all | solution.py:65
where the time goes:
time: 228 us; the launch traced here: 227 us
  waiting for transfers between devices  145 us (64%)
  starting transfers between devices  32.1 us (14%)
  other arithmetic  17.3 us (8%)
  local copies, waits for them, and re-layouts  14.8 us (6%)
  matrix products  9.98 us (4%)
  blocking collectives  8.11 us (4%)
    all_to_all x1, waiting for transfers between devices, on_device(): lax.all_to_all(code_rows, 'seq', split_axis=0, concat_axis=1, tiled=True)  95 us
    all_to_all x1, waiting for transfers between devices, on_device(): lax.all_to_all(packed[0], 'grp', split_axis=1, concat_axis=0, tiled=True)  47.7 us
    all_to_all x1, starting transfers between devices, on_device(): lax.all_to_all(id_rows, 'seq', split_axis=0, concat_axis=1, tiled=True)  13.7 us
    all_to_all x1, starting transfers between devices, on_device(): lax.all_to_all(code_rows, 'seq', split_axis=0, concat_axis=1, tiled=True)  10.3 us
    dot_general x1, matrix products, block_prefix(): jnp.einsum('tu,ruc->rtc', lower_ones, deltas, precision=lax.Precision.HIG...  9.38 us
    all_to_all x1, blocking collectives, on_device(): lax.all_to_all(packed[1], 'grp', split_axis=1, concat_axis=0, tiled=True)  8.11 us
    mul x1, other arithmetic, dequantize(): return (shaped * scales[..., :, None, :]).reshape(code_vals.shape)  6.73 us
    convert_element_type x1, other arithmetic, on_device(): delta_codes.astype(jnp.bfloat16)  6.38 us
  transfers between devices with their start and end apart: 4, of which 3 were waited for; matrix products, arithmetic and copies ran while one was open for 5% of the time, Pallas kernels for 0%

commit v1 on v0

v1 whole, which is shorter than its diff:
```python
import functools

import jax
import jax.numpy as jnp
from jax import lax
from jax.experimental import pallas as pl
from jax.experimental.pallas import tpu as pltpu
from jax.sharding import PartitionSpec as P

MESH = pl.DeviceIdType.MESH
NX, NY, NZ = 4, 4, 8
SLOTS = 4
ROUNDS = 16


def rounds_of(r):
    if r >= 14:
        return 0, 15 - r
    if r >= 12:
        return 4, r - 12
    return (r // 4 + 1) * (1 - 2 * (r % 2)), (r // 2) % 2


def exchange_kernel(
    codes, ids, anchors, anchor_scale, out, ids_out, anchor_out,
    stage, tri, summed, passed, id_src, id_pass, id_got,
    stage_sem, y_send, y_recv, f_send, f_recv, iy_send, iy_recv, if_send, if_recv, own_sem,
):
    s = lax.axis_index("seq")
    y = lax.axis_index("grp")
    core = s % 2
    z = (s // 2) % NZ
    x = s // (2 * NZ)
    here = z * 2 + core

    barrier = pltpu.get_barrier_semaphore()

    def greet(j, _):
        pl.semaphore_signal(barrier, inc=1, device_id=((s + j) % 64, y), device_id_type=MESH)
        return 0

    for k in range(1, NY):
        pl.semaphore_signal(barrier, inc=1, device_id=(s, (y + k) % NY), device_id_type=MESH)
    lax.fori_loop(1, 64, greet, 0)

    def fetch(n, slot):
        return pltpu.make_async_copy(
            codes.at[n // 4, pl.ds((n % 4) * 4, 4)], stage.at[slot], stage_sem.at[slot]
        )

    for n in range(SLOTS):
        fetch(n, n).start()

    levels = ids[...].astype(jnp.float32).reshape(64, 16)
    lane = lax.broadcasted_iota(jnp.int32, (16, 128), 1)
    entry = lax.broadcasted_iota(jnp.int32, (16, 128), 0)
    place = (lane == entry + (s % 8) * 16).astype(jnp.float32)
    spread = jnp.dot(levels, place, preferred_element_type=jnp.float32)
    for b in range(4):
        for k in range(16):
            id_src[k // 4, b * 4 + k % 4] = spread[b * 16 + k : b * 16 + k + 1, :]
    row_scale = anchor_scale[...]
    for h in range(4):
        id_src[h, 16] = anchors[here // 4, pl.ds(h * 4 + here % 4, 1), :].astype(jnp.float32) * row_scale

    row = lax.broadcasted_iota(jnp.int32, (256, 256), 0)
    col = lax.broadcasted_iota(jnp.int32, (256, 256), 1)
    tri[...] = ((row // 16 == col // 16) & (col <= row)).astype(jnp.float32).astype(jnp.bfloat16)

    def prefix(n, _):
        slot = n % SLOTS
        fetch(n, slot).wait()
        for q in range(0, 4, 2):
            pair = jnp.concatenate(
                [stage[slot, q].astype(jnp.float32), stage[slot, q + 1].astype(jnp.float32)], axis=1
            ).astype(jnp.bfloat16)
            sums = jnp.dot(tri[...], pair, preferred_element_type=jnp.float32).astype(jnp.bfloat16)
            summed[n % 4, (n // 4) * 4 + q] = sums[:, :128]
            summed[n % 4, (n // 4) * 4 + q + 1] = sums[:, 128:]

        @pl.when(n + SLOTS < 16)
        def _():
            fetch(n + SLOTS, slot).start()

        return 0

    lax.fori_loop(0, 16, prefix, 0)
    pl.semaphore_wait(barrier, 66)

    def target(r):
        dz, other = rounds_of(r)
        to_z = (z + dz + NZ) % NZ
        to_core = (core + other) % 2
        return to_z, to_core, to_z * 2 + to_core

    for k in range(1, NY):
        pltpu.make_async_remote_copy(
            src_ref=id_src.at[(y + k) % NY], dst_ref=id_pass.at[k - 1],
            send_sem=iy_send, recv_sem=iy_recv.at[k - 1],
            device_id=(s, (y + k) % NY), device_id_type=MESH,
        ).start()
    def send_y(r):
        _, _, m = target(r)
        for k in range(1, NY):
            pltpu.make_async_remote_copy(
                src_ref=summed.at[(y + k) % NY, m], dst_ref=passed.at[k - 1, r],
                send_sem=y_send, recv_sem=y_recv.at[k - 1, r],
                device_id=(s, (y + k) % NY), device_id_type=MESH,
            ).start()

    def send_final(r, k):
        to_z, to_core, m = target(r)
        to_x = (y - k + NX) % NX
        src = summed.at[y, m] if k == 0 else passed.at[k - 1, r]
        id_row = id_src.at[y, m] if k == 0 else id_pass.at[k - 1, m]

        def remote():
            where = ((to_x * NZ + to_z) * 2 + to_core, y)
            pltpu.make_async_remote_copy(
                src_ref=id_row, dst_ref=id_got.at[s], send_sem=if_send, recv_sem=if_recv,
                device_id=where, device_id_type=MESH,
            ).start()
            pltpu.make_async_remote_copy(
                src_ref=src, dst_ref=out.at[s], send_sem=f_send, recv_sem=f_recv,
                device_id=where, device_id_type=MESH,
            ).start()

        if r < 15:
            remote()
        else:
            pl.when(to_x != x)(remote)

            @pl.when(to_x == x)
            def _():
                id_got[s] = id_row[...]
                anchor_out[...] = (id_src[y, 16] if k == 0 else id_pass[k - 1, 16])
                pltpu.make_async_copy(src, out.at[s], own_sem).start()

    LEAD = 4
    for r in range(LEAD):
        send_y(r)
    for r in range(LEAD):
        send_final(r, 0)
    for r in range(LEAD, ROUNDS):
        send_y(r)
    for k in range(1, NY):
        pltpu.make_async_copy(id_pass.at[k - 1], id_pass.at[k - 1], iy_recv.at[k - 1]).wait()
    for r in range(ROUNDS):
        for k in range(1, NY):
            pltpu.make_async_copy(passed.at[k - 1, r], passed.at[k - 1, r], y_recv.at[k - 1, r]).wait()
            send_final(r, k)
        if r + LEAD < ROUNDS:
            send_final(r + LEAD, 0)

    pltpu.make_async_copy(id_got.at[pl.ds(0, 63)], id_got.at[pl.ds(0, 63)], if_recv).wait()
    for j in range(8):
        ids_out[pl.ds(j, 1), :] = functools.reduce(jnp.add, [id_got[j * 8 + i] for i in range(8)])
    pltpu.make_async_copy(out.at[0], out.at[0], own_sem).wait()
    pltpu.make_async_copy(passed, passed, y_send).wait()
    pltpu.make_async_copy(id_pass, id_pass, iy_send).wait()
    pltpu.make_async_copy(id_got.at[pl.ds(0, 63)], id_got.at[pl.ds(0, 63)], if_send).wait()
    pltpu.make_async_copy(out.at[pl.ds(0, 63)], out.at[pl.ds(0, 63)], f_send).wait()
    pltpu.make_async_copy(out.at[pl.ds(0, 63)], out.at[pl.ds(0, 63)], f_recv).wait()


def exchange(codes, ids, anchors, anchor_scale):
    vmem = pl.BlockSpec(memory_space=pltpu.VMEM)
    hbm = pl.BlockSpec(memory_space=pl.ANY)
    return pl.pallas_call(
        exchange_kernel,
        out_shape=(
            jax.ShapeDtypeStruct((64, 256, 128), jnp.bfloat16),
            jax.ShapeDtypeStruct((8, 128), jnp.float32),
            jax.ShapeDtypeStruct((1, 128), jnp.float32),
        ),
        in_specs=[hbm, vmem, vmem, vmem],
        out_specs=(hbm, vmem, vmem),
        scratch_shapes=[
            pltpu.VMEM((SLOTS, 4, 256, 128), jnp.int32),
            pltpu.VMEM((256, 256), jnp.bfloat16),
            pltpu.VMEM((4, 16, 256, 128), jnp.bfloat16),
            pltpu.VMEM((3, 16, 256, 128), jnp.bfloat16),
            pltpu.VMEM((4, 17, 1, 128), jnp.float32),
            pltpu.VMEM((3, 17, 1, 128), jnp.float32),
            pltpu.VMEM((64, 1, 128), jnp.float32),
            pltpu.SemaphoreType.DMA((SLOTS,)),
            pltpu.SemaphoreType.DMA,
            pltpu.SemaphoreType.DMA((3, ROUNDS)),
            pltpu.SemaphoreType.DMA,
            pltpu.SemaphoreType.DMA,
            pltpu.SemaphoreType.DMA,
            pltpu.SemaphoreType.DMA((3,)),
            pltpu.SemaphoreType.DMA,
            pltpu.SemaphoreType.DMA,
            pltpu.SemaphoreType.DMA,
        ],
        compiler_params=pltpu.CompilerParams(
            collective_id=0, has_side_effects=True, vmem_limit_bytes=40 * 2**20
        ),
        name="exchange",
    )(codes, ids, anchors, anchor_scale)


def rebuild_kernel(codes, ids, table, anchor, out, values, scales, carries, carry):
    step = pl.program_id(0)

    @pl.when(step == 0)
    def _():
        carry[...] = anchor[...]

    wanted = ids[pl.ds(step, 1), :]
    entry = lax.broadcasted_iota(jnp.int32, (16, 128), 0).astype(jnp.float32)
    onehot = (entry == wanted).astype(jnp.float32)
    scales[...] = lax.dot_general(
        onehot, table[...], (((0,), (0,)), ((), ())),
        precision=lax.Precision.HIGHEST, preferred_element_type=jnp.float32,
    )
    for j in range(128):
        block = codes[j // 16, pl.ds((j % 16) * 16, 16), :].astype(jnp.float32)
        values[pl.ds(j * 16, 16), :] = block * scales[pl.ds(j, 1), :]
    ends = values[pl.ds(15, 128, stride=16), :]
    row = lax.broadcasted_iota(jnp.int32, (128, 128), 0)
    col = lax.broadcasted_iota(jnp.int32, (128, 128), 1)
    strict = (col < row).astype(jnp.float32)
    before = jnp.dot(strict, ends, precision=lax.Precision.HIGHEST, preferred_element_type=jnp.float32)
    carries[...] = before + carry[...]
    carry[...] = carries[127:128, :] + ends[127:128, :]
    for j in range(128):
        block = values[pl.ds(j * 16, 16), :] + carries[pl.ds(j, 1), :]
        out[pl.ds(j * 16, 16), :] = block.astype(jnp.bfloat16)


def rebuild(codes, ids, table, anchor):
    return pl.pallas_call(
        rebuild_kernel,
        grid=(8,),
        out_shape=jax.ShapeDtypeStruct((16384, 128), jnp.bfloat16),
        in_specs=[
            pl.BlockSpec((8, 256, 128), lambda i: (i, 0, 0)),
            pl.BlockSpec((8, 128), lambda i: (0, 0)),
            pl.BlockSpec((16, 128), lambda i: (0, 0)),
            pl.BlockSpec((1, 128), lambda i: (0, 0)),
        ],
        out_specs=pl.BlockSpec((2048, 128), lambda i: (i, 0)),
        scratch_shapes=[
            pltpu.VMEM((2048, 128), jnp.float32),
            pltpu.VMEM((128, 128), jnp.float32),
            pltpu.VMEM((128, 128), jnp.float32),
            pltpu.VMEM((1, 128), jnp.float32),
        ],
        name="rebuild",
    )(codes, ids, table, anchor)


def on_device(delta_codes, scale_index, anchor_codes, scale_table, anchor_scale):
    codes, ids, anchor = exchange(delta_codes, scale_index, anchor_codes, anchor_scale.reshape(1, 128))
    return rebuild(codes, ids, scale_table, anchor).reshape(1, 1, 16384, 128)


def solution(mesh):
    placed = (P("grp", None, "seq", None), P("grp", None, "seq"), P("grp", None, None), P(), P())
    return jax.shard_map(
        on_device,
        mesh=mesh,
        in_specs=placed,
        out_specs=P("grp", "seq", None, None),
        check_vma=False,
    )
```

time: 228 us -> 130 us (0.57)
  waiting for transfers between devices: 145 us -> 0 us
  Pallas kernels: 0 us -> 121 us
  starting transfers between devices: 32.1 us -> 0 us
  other arithmetic: 17.3 us -> 0 us
  matrix products: 9.98 us -> 0 us
  blocking collectives: 8.11 us -> 0 us
  local copies, waits for them, and re-layouts: 14.8 us -> 8.59 us
    all_to_all x4 -> x0, waiting for transfers between devices: 145 us -> none  [the longest x1 95 us: on_device(): lax.all_to_all(code_rows, 'seq', split_axis=0, concat_axis=1, tiled=True)]
    pallas_call x0 -> x2, Pallas kernels: none -> 121 us  [the longest x1 112 us: exchange(): pl.pallas_call(exchange_kernel, out_shape=(jax.ShapeDtypeStruct((64, 256,...]
    all_to_all x4 -> x0, starting transfers between devices: 32.1 us -> none  [the longest x1 13.7 us: on_device(): lax.all_to_all(id_rows, 'seq', split_axis=0, concat_axis=1, tiled=True)]
    dot_general x3 -> x0, matrix products: 9.98 us -> none  [the longest x1 9.38 us: block_prefix(): jnp.einsum('tu,ruc->rtc', lower_ones, deltas, precision=lax.Precision.HIG...]
    convert_element_type x4 -> x0, other arithmetic: 9.75 us -> none  [the longest x1 6.38 us: on_device(): delta_codes.astype(jnp.bfloat16)]
    unnamed x8 -> x14, local copies, waits for them, and re-layouts: 0.19 us -> 8.59 us
    all_to_all x1 -> x0, blocking collectives: 8.11 us -> none  [on_device(): lax.all_to_all(packed[1], 'grp', split_axis=1, concat_axis=0, tiled=True)]
    mul x1 -> x0, other arithmetic: 6.73 us -> none  [dequantize(): return (shaped * scales[..., :, None, :]).reshape(code_vals.shape)]
  transfers between devices with their start and end apart: 4 -> 0, of which waited for: 3 -> 0; matrix products, arithmetic and copies ran while one was open for 5% -> 0% of each run, Pallas kernels for 0% -> 0%
where the time goes in v1:
time: 130 us
  Pallas kernels  121 us (93%)
  local copies, waits for them, and re-layouts  8.59 us (7%)
    pallas_call x1, Pallas kernels, exchange(): pl.pallas_call(exchange_kernel, out_shape=(jax.ShapeDtypeStruct((64, 256,...  112 us
    pallas_call x1, Pallas kernels, rebuild(): pl.pallas_call(rebuild_kernel, grid=(8,), out_shape=jax.ShapeDtypeStruct(...  9.11 us
    unnamed x14, local copies, waits for them, and re-layouts  8.59 us

profile of v1, /device:TPU:3, one launch (start us, length us, event | category | flops | bytes accessed | tf_op | source)
XLA Modules:
  0.0 130.1 jit_solution(8387073192940063339)
XLA Ops:
  0.0 0.0 copy-start
  0.0 3.4 %copy-done = s32[4,16,256,128]{3,2,1,0:T(8,128)S(1)} copy-done((s32[4,16,256,128]{3,2,1,0:T(8,128)S(1)}, s32[4,16,256,128]{3,2,1,0:T(8,128)}, u32[]{:S(2)}) %copy-start) | copy-done | bytes 8388632
  3.4 0.0 copy-start.2
  3.4 0.8 copy-done.2
  4.1 0.0 copy-start.3
  4.1 0.8 copy-done.3
  4.9 0.0 copy-start.5
  4.9 0.7 copy-done.5
  5.6 112.3 %exchange.1 = (bf16[64,256,128]{2,1,0:T(8,128)(2,1)S(1)}, f32[8,128]{1,0:T(8,128)S(1)}, f32[1,128]{1,0:T(1,128)S(1)}) custom-call(s32[4,16,256,128]{3,2,1,0:T(8,128)S(1)} %copy-done, s32[4,16,16]{2,1,0:T(8,128)S(1)} %copy-done.2, s32[4,16,128]{2,1,0:T(8,128)S(1)} %copy-done.3, f32[1,128]{1,0:T(1,128)S(1)} %bitcast.2), custom_call_target="tpu_custom_call" | custom-call | tf_op jit(solution)/shard_map/exchange/pallas_call | solution.py:169
  117.9 0.0 copy-start.1
  117.9 1.9 %copy-done.1 = bf16[64,256,128]{2,1,0:T(8,128)(2,1)} copy-done((bf16[64,256,128]{2,1,0:T(8,128)(2,1)}, bf16[64,256,128]{2,1,0:T(8,128)(2,1)S(1)}, u32[]{:S(2)}) %copy-start.1) | copy-done | bytes 4194328
  119.9 0.0 copy-start.4
  119.9 0.6 copy-done.4
  120.4 0.0 copy-start.6
  120.4 0.5 copy-done.6
  121.0 9.1 %rebuild.1 = bf16[16384,128]{1,0:T(8,128)(2,1)} custom-call(bf16[64,256,128]{2,1,0:T(8,128)(2,1)} %copy-done.1, f32[8,128]{1,0:T(8,128)} %copy-done.4, f32[16,128]{1,0:T(8,128)} %table.1, f32[1,128]{1,0:T(1,128)} %copy-done.6), custom_call_target="tpu_custom_call" | custom-call | tf_op jit(solution)/shard_map/rebuild/pallas_call | solution.py:234
Async XLA Ops:
  0.0 3.4 %copy-start = (s32[4,16,256,128]{3,2,1,0:T(8,128)S(1)}, s32[4,16,256,128]{3,2,1,0:T(8,128)}, u32[]{:S(2)}) copy-start(s32[4,16,256,128]{3,2,1,0:T(8,128)} %codes.1) | copy-start | bytes 25165828
  3.4 0.8 copy-start.2
  4.1 0.8 copy-start.3
  4.9 0.7 copy-start.5
  117.9 1.9 %copy-start.1 = (bf16[64,256,128]{2,1,0:T(8,128)(2,1)}, bf16[64,256,128]{2,1,0:T(8,128)(2,1)S(1)}, u32[]{:S(2)}) copy-start(bf16[64,256,128]{2,1,0:T(8,128)(2,1)S(1)} %get-tuple-element.8.codes) | copy-start | bytes 12582916
  119.9 0.6 copy-start.4
  120.4 0.5 copy-start.6

commit v2 on v1

v2 whole, which is shorter than its diff:
```python
import functools

import jax
import jax.numpy as jnp
from jax import lax
from jax.experimental import pallas as pl
from jax.experimental.pallas import tpu as pltpu
from jax.sharding import PartitionSpec as P

MESH = pl.DeviceIdType.MESH
NX, NY, NZ = 4, 4, 8
SLOTS = 4
ROUNDS = 16
LEAD = 2
PIECES = 8


ORDER = [(4, 0), (4, 1), (3, 0), (-3, 0), (3, 1), (-3, 1), (2, 0), (-2, 0), (2, 1), (-2, 1), (1, 0), (-1, 0), (1, 1), (-1, 1), (0, 1), (0, 0)]


def rounds_of(r):
    return ORDER[r]


def exchange_kernel(
    codes, ids_hbm, anchors_hbm, row_scale_hbm, table_hbm, grown, totals, anchor_out,
    stage, tri, blocks, landed, scales, ids, anchors, row_scale, table, id_rows, id_got,
    stage_sem, small_sem, y_send, y_recv, f_send, f_recv, iy_send, iy_recv, if_send, if_recv, own_sem,
):
    s = lax.axis_index("seq")
    y = lax.axis_index("grp")
    core = s % 2
    z = (s // 2) % NZ
    x = s // (2 * NZ)
    here = z * 2 + core

    def fetch(n, slot):
        return pltpu.make_async_copy(
            codes.at[n // 4, pl.ds((n % 4) * 4, 4)], stage.at[slot], stage_sem.at[slot]
        )

    for n in range(SLOTS):
        fetch(n, n).start()
    small = [
        pltpu.make_async_copy(ids_hbm, ids, small_sem.at[0]),
        pltpu.make_async_copy(anchors_hbm, anchors, small_sem.at[1]),
        pltpu.make_async_copy(row_scale_hbm, row_scale, small_sem.at[2]),
        pltpu.make_async_copy(table_hbm, table, small_sem.at[3]),
    ]
    for copy in small:
        copy.start()

    barrier = pltpu.get_barrier_semaphore()

    def greet(j, _):
        pl.semaphore_signal(barrier, inc=1, device_id=((s + j) % 64, y), device_id_type=MESH)
        return 0

    for k in range(1, NY):
        pl.semaphore_signal(barrier, inc=1, device_id=(s, (y + k) % NY), device_id_type=MESH)
    lax.fori_loop(1, 64, greet, 0)

    row = lax.broadcasted_iota(jnp.int32, (256, 256), 0)
    col = lax.broadcasted_iota(jnp.int32, (256, 256), 1)
    tri[...] = ((row // 16 == col // 16) & (col <= row)).astype(jnp.float32).astype(jnp.bfloat16)

    def prefix(n, _):
        slot = n % SLOTS
        fetch(n, slot).wait()
        for q in range(0, 4, 2):
            pair = jnp.concatenate(
                [stage[slot, q].astype(jnp.float32), stage[slot, q + 1].astype(jnp.float32)], axis=1
            ).astype(jnp.bfloat16)
            sums = jnp.dot(tri[...], pair, preferred_element_type=jnp.float32).astype(jnp.bfloat16)
            blocks[n % 4, (n // 4) * 4 + q] = sums[:, :128]
            blocks[n % 4, (n // 4) * 4 + q + 1] = sums[:, 128:]

        @pl.when(n + SLOTS < 16)
        def _():
            fetch(n + SLOTS, slot).start()

        return 0

    lax.fori_loop(0, 16, prefix, 0)

    for copy in small:
        copy.wait()
    levels = ids[...].astype(jnp.float32).reshape(64, 16)
    lane = lax.broadcasted_iota(jnp.int32, (16, 128), 1)
    entry = lax.broadcasted_iota(jnp.int32, (16, 128), 0)
    place = (lane == entry + (s % 8) * 16).astype(jnp.float32)
    spread = jnp.dot(levels, place, preferred_element_type=jnp.float32)
    for b in range(4):
        for k in range(16):
            id_rows[k // 4, b * 4 + k % 4] = spread[b * 16 + k : b * 16 + k + 1, :]
    for h in range(4):
        id_rows[h, 16] = (
            anchors[here // 4, pl.ds(h * 4 + here % 4, 1), :].astype(jnp.float32) * row_scale[...]
        )
    pl.semaphore_wait(barrier, 66)

    def target(r):
        dz, other = rounds_of(r)
        to_z = (z + dz + NZ) % NZ
        to_core = (core + other) % 2
        return to_z, to_core, to_z * 2 + to_core

    def slot_of(k):
        return jnp.where(k == 0, y, 3 + k)

    def pass_on(r):
        _, _, m = target(r)
        for k in (1, 3, 2):
            pltpu.make_async_remote_copy(
                src_ref=blocks.at[(y + k) % NY, m], dst_ref=blocks.at[3 + k, m],
                send_sem=y_send, recv_sem=y_recv.at[k - 1, r],
                device_id=(s, (y + k) % NY), device_id_type=MESH,
            ).start()

    def send(r, k, src, dst, send_sem, recv_sem):
        to_z, to_core, _ = target(r)
        to_x = (y - k + NX) % NX

        def remote():
            pltpu.make_async_remote_copy(
                src_ref=src, dst_ref=dst, send_sem=send_sem, recv_sem=recv_sem,
                device_id=((to_x * NZ + to_z) * 2 + to_core, y), device_id_type=MESH,
            ).start()

        if ORDER[r] == (0, 0):
            pl.when(to_x != x)(remote)
        else:
            remote()

    def send_block(r, k):
        send(r, k, blocks.at[slot_of(k), target(r)[2]], landed.at[s], f_send, f_recv.at[s])

    def send_ids(r, k):
        send(r, k, id_rows.at[slot_of(k), target(r)[2]], id_got.at[s], if_send, if_recv)

    for k in range(1, NY):
        pltpu.make_async_remote_copy(
            src_ref=id_rows.at[(y + k) % NY], dst_ref=id_rows.at[3 + k],
            send_sem=iy_send, recv_sem=iy_recv.at[k - 1],
            device_id=(s, (y + k) % NY), device_id_type=MESH,
        ).start()
    for r in range(LEAD):
        pass_on(r)
        send_block(r, 0)
    for r in range(LEAD, ROUNDS):
        pass_on(r)
    for k in range(1, NY):
        pltpu.make_async_copy(id_rows.at[3 + k], id_rows.at[3 + k], iy_recv.at[k - 1]).wait()
    for r in range(ROUNDS):
        for k in range(NY):
            send_ids(r, k)
    own = slot_of((y - x + NX) % NX)
    id_got[s] = id_rows[own, here]
    anchor_out[...] = id_rows[own, 16]
    for r in range(ROUNDS):
        for i in range(NX):
            k = (y - x - i - 2 * core - (1 if ORDER[r][0] < 0 else 0) + 12) % 4
            if r + LEAD < ROUNDS:
                pl.when(k == 0)(functools.partial(send_block, r + LEAD, 0))

            @pl.when(k != 0)
            def _():
                pltpu.make_async_copy(blocks.at[3 + k, 0], blocks.at[3 + k, 0], y_recv.at[k - 1, r]).wait()
                send_block(r, k)

    pltpu.make_async_copy(id_got.at[pl.ds(0, 63)], id_got.at[pl.ds(0, 63)], if_recv).wait()
    entry = lax.broadcasted_iota(jnp.int32, (16, 128), 0).astype(jnp.float32)
    for j in range(8):
        wanted = functools.reduce(jnp.add, [id_got[j * 8 + i] for i in range(8)])
        scales[pl.ds(j * 128, 128), :] = lax.dot_general(
            (entry == wanted).astype(jnp.float32), table[...], (((0,), (0,)), ((), ())),
            precision=lax.Precision.HIGHEST, preferred_element_type=jnp.float32,
        )

    def grow(block, at):
        run = jnp.zeros((1, 128), jnp.float32)
        for j in range(16):
            v = block[pl.ds(j * 16, 16), :].astype(jnp.float32) * scales[pl.ds(at * 16 + j, 1), :]
            grown[at, pl.ds(j * 16, 16), :] = v + run
            run = run + v[15:16, :]
        totals[pl.ds(at, 1), :] = run

    grow(blocks.at[own, here], s)

    for r in range(ROUNDS):
        dz, other = rounds_of(r)

        def take(j, _):
            from_x = (x + j) % NX
            at = (from_x * NZ + (z - dz + NZ) % NZ) * 2 + (core + other) % 2
            pltpu.make_async_copy(landed.at[at], landed.at[at], f_recv.at[at]).wait()
            grow(landed.at[at], at)
            return 0

        lax.fori_loop(1 if ORDER[r] == (0, 0) else 0, NX, take, 0)

    pltpu.make_async_copy(blocks.at[pl.ds(4, 3)], blocks.at[pl.ds(4, 3)], y_send).wait()
    pltpu.make_async_copy(id_rows.at[pl.ds(4, 3)], id_rows.at[pl.ds(4, 3)], iy_send).wait()
    pltpu.make_async_copy(id_got.at[pl.ds(0, 63)], id_got.at[pl.ds(0, 63)], if_send).wait()
    pltpu.make_async_copy(landed.at[pl.ds(0, 63)], landed.at[pl.ds(0, 63)], f_send).wait()


def exchange(codes, ids, anchors, anchor_scale, table):
    vmem = pl.BlockSpec(memory_space=pltpu.VMEM)
    hbm = pl.BlockSpec(memory_space=pltpu.HBM)
    return pl.pallas_call(
        exchange_kernel,
        out_shape=(
            jax.ShapeDtypeStruct((64, 256, 128), jnp.float32),
            jax.ShapeDtypeStruct((64, 128), jnp.float32),
            jax.ShapeDtypeStruct((1, 128), jnp.float32),
        ),
        in_specs=[hbm] * 5,
        out_specs=(vmem, vmem, vmem),
        scratch_shapes=[
            pltpu.VMEM((SLOTS, 4, 256, 128), jnp.int32),
            pltpu.VMEM((256, 256), jnp.bfloat16),
            pltpu.VMEM((7, 16, 256, 128), jnp.bfloat16),
            pltpu.VMEM((64, 256, 128), jnp.bfloat16),
            pltpu.VMEM((1024, 128), jnp.float32),
            pltpu.VMEM((4, 16, 16), jnp.int32),
            pltpu.VMEM((4, 16, 128), jnp.int32),
            pltpu.VMEM((1, 128), jnp.float32),
            pltpu.VMEM((16, 128), jnp.float32),
            pltpu.VMEM((7, 17, 1, 128), jnp.float32),
            pltpu.VMEM((64, 1, 128), jnp.float32),
            pltpu.SemaphoreType.DMA((SLOTS,)),
            pltpu.SemaphoreType.DMA((4,)),
            pltpu.SemaphoreType.DMA,
            pltpu.SemaphoreType.DMA((3, ROUNDS)),
            pltpu.SemaphoreType.DMA,
            pltpu.SemaphoreType.DMA((64,)),
            pltpu.SemaphoreType.DMA,
            pltpu.SemaphoreType.DMA((3,)),
            pltpu.SemaphoreType.DMA,
            pltpu.SemaphoreType.DMA,
            pltpu.SemaphoreType.DMA,
        ],
        compiler_params=pltpu.CompilerParams(
            collective_id=0, has_side_effects=True, vmem_limit_bytes=18 * 2**20
        ),
        name="exchange",
    )(*[pltpu.with_memory_space_constraint(a, pltpu.HBM) for a in (codes, ids, anchors, anchor_scale, table)])


def finish_kernel(grown, totals, anchor, out, rounded, sem):
    carry = anchor[...]
    copies = []
    for n in range(PIECES):
        blocks = 64 // PIECES

        def add(i, carry):
            at = n * blocks + i
            rounded[at] = (grown[at] + carry).astype(jnp.bfloat16)
            return carry + totals[pl.ds(at, 1), :]

        carry = lax.fori_loop(0, blocks, add, carry)
        piece = pl.ds(n * blocks, blocks)
        copies.append(pltpu.make_async_copy(rounded.at[piece], out.at[piece], sem.at[n]))
        copies[-1].start()
    for copy in copies:
        copy.wait()


def finish(grown, totals, anchor):
    vmem = pl.BlockSpec(memory_space=pltpu.VMEM)
    return pl.pallas_call(
        finish_kernel,
        out_shape=jax.ShapeDtypeStruct((64, 256, 128), jnp.bfloat16),
        in_specs=[vmem, vmem, vmem],
        out_specs=pl.BlockSpec(memory_space=pltpu.HBM),
        scratch_shapes=[
            pltpu.VMEM((64, 256, 128), jnp.bfloat16),
            pltpu.SemaphoreType.DMA((PIECES,)),
        ],
        compiler_params=pltpu.CompilerParams(vmem_limit_bytes=6 * 2**20),
        name="finish",
    )(grown, totals, anchor)


def on_device(delta_codes, scale_index, anchor_codes, scale_table, anchor_scale):
    grown, totals, anchor = exchange(
        delta_codes, scale_index, anchor_codes, anchor_scale.reshape(1, 128), scale_table
    )
    return finish(grown, totals, anchor).reshape(1, 1, 16384, 128)


def solution(mesh):
    placed = (P("grp", None, "seq", None), P("grp", None, "seq"), P("grp", None, None), P(), P())
    return jax.shard_map(
        on_device,
        mesh=mesh,
        in_specs=placed,
        out_specs=P("grp", "seq", None, None),
        check_vma=False,
    )
```

time: 130 us -> 111 us (0.85); the launches traced: 130 us -> 110 us
  Pallas kernels: 121 us -> 109 us
  local copies, waits for them, and re-layouts: 8.59 us -> 0 us
    unnamed x14 -> x0, local copies, waits for them, and re-layouts: 8.59 us -> none
    pallas_call x1, Pallas kernels: 9.11 us -> 2.16 us  [finish(): pl.pallas_call(finish_kernel, out_shape=jax.ShapeDtypeStruct((64, 256, 12...]
    pallas_call x1, Pallas kernels: 112 us -> 107 us  [exchange(): pl.pallas_call(exchange_kernel, out_shape=(jax.ShapeDtypeStruct((64, 256,...]
where the time goes in v2:
time: 111 us; the launch traced here: 110 us
  Pallas kernels  109 us (98%)
    pallas_call x1, Pallas kernels, exchange(): pl.pallas_call(exchange_kernel, out_shape=(jax.ShapeDtypeStruct((64, 256,...  107 us

profile of v2, /device:TPU:3, one launch (start us, length us, event | category | flops | bytes accessed | tf_op | source)
XLA Modules:
  0.0 109.5 jit_solution(8745716959804664781)
XLA Ops:
  0.0 107.3 %exchange.1 = (f32[64,256,128]{2,1,0:T(8,128)S(1)}, f32[64,128]{1,0:T(8,128)S(1)}, f32[1,128]{1,0:T(1,128)S(1)}) custom-call(s32[4,16,256,128]{3,2,1,0:T(8,128)} %codes.1, s32[4,16,16]{2,1,0:T(8,128)} %ids_hbm.1, s32[4,16,128]{2,1,0:T(8,128)} %anchors_hbm.1, f32[1,128]{1,0:T(1,128)} %bitcast.2, f32[16,128]{1,0:T(8,128)} %table_hbm.1), custom_call_target="tpu_custom_call" | custom-call | tf_op jit(solution)/shard_map/exchange/pallas_call | solution.py:211
  107.3 2.2 %finish.1 = bf16[64,256,128]{2,1,0:T(8,128)(2,1)} custom-call(f32[64,256,128]{2,1,0:T(8,128)S(1)} %get-tuple-element.8.grown, f32[64,128]{1,0:T(8,128)S(1)} %get-tuple-element.9.totals, f32[1,128]{1,0:T(1,128)S(1)} %get-tuple-element.10.anchor), custom_call_target="tpu_custom_call" | custom-call | tf_op jit(solution)/shard_map/finish/pallas_call | solution.py:272

commit v3 on v2

--- a/solution.py
+++ b/solution.py
@@ -12,6 +12,8 @@
 SLOTS = 4
 ROUNDS = 16
 LEAD = 2
+AHEAD = 2
+IDS_AT = 3
 PIECES = 8
 
 
@@ -34,13 +36,20 @@
     x = s // (2 * NZ)
     here = z * 2 + core
 
-    def fetch(n, slot):
+    def target(r):
+        dz, other = rounds_of(r)
+        to_z = (z + dz + NZ) % NZ
+        to_core = (core + other) % 2
+        return to_z, to_core, to_z * 2 + to_core
+
+    def fetch(r):
+        m = target(r)[2]
         return pltpu.make_async_copy(
-            codes.at[n // 4, pl.ds((n % 4) * 4, 4)], stage.at[slot], stage_sem.at[slot]
+            codes.at[m // 4, :, m % 4], stage.at[r % SLOTS], stage_sem.at[r % SLOTS]
         )
 
-    for n in range(SLOTS):
-        fetch(n, n).start()
+    for r in range(SLOTS):
+        fetch(r).start()
     small = [
         pltpu.make_async_copy(ids_hbm, ids, small_sem.at[0]),
         pltpu.make_async_copy(anchors_hbm, anchors, small_sem.at[1]),
@@ -64,46 +73,34 @@
     col = lax.broadcasted_iota(jnp.int32, (256, 256), 1)
     tri[...] = ((row // 16 == col // 16) & (col <= row)).astype(jnp.float32).astype(jnp.bfloat16)
 
-    def prefix(n, _):
-        slot = n % SLOTS
-        fetch(n, slot).wait()
-        for q in range(0, 4, 2):
+    def prefix(r):
+        m = target(r)[2]
+        fetch(r).wait()
+        for h in range(0, 4, 2):
             pair = jnp.concatenate(
-                [stage[slot, q].astype(jnp.float32), stage[slot, q + 1].astype(jnp.float32)], axis=1
+                [stage[r % SLOTS, h].astype(jnp.float32), stage[r % SLOTS, h + 1].astype(jnp.float32)], axis=1
             ).astype(jnp.bfloat16)
             sums = jnp.dot(tri[...], pair, preferred_element_type=jnp.float32).astype(jnp.bfloat16)
-            blocks[n % 4, (n // 4) * 4 + q] = sums[:, :128]
-            blocks[n % 4, (n // 4) * 4 + q + 1] = sums[:, 128:]
-
-        @pl.when(n + SLOTS < 16)
-        def _():
-            fetch(n + SLOTS, slot).start()
-
-        return 0
-
-    lax.fori_loop(0, 16, prefix, 0)
-
-    for copy in small:
-        copy.wait()
-    levels = ids[...].astype(jnp.float32).reshape(64, 16)
-    lane = lax.broadcasted_iota(jnp.int32, (16, 128), 1)
-    entry = lax.broadcasted_iota(jnp.int32, (16, 128), 0)
-    place = (lane == entry + (s % 8) * 16).astype(jnp.float32)
-    spread = jnp.dot(levels, place, preferred_element_type=jnp.float32)
-    for b in range(4):
-        for k in range(16):
-            id_rows[k // 4, b * 4 + k % 4] = spread[b * 16 + k : b * 16 + k + 1, :]
-    for h in range(4):
-        id_rows[h, 16] = (
-            anchors[here // 4, pl.ds(h * 4 + here % 4, 1), :].astype(jnp.float32) * row_scale[...]
-        )
-    pl.semaphore_wait(barrier, 66)
-
-    def target(r):
-        dz, other = rounds_of(r)
-        to_z = (z + dz + NZ) % NZ
-        to_core = (core + other) % 2
-        return to_z, to_core, to_z * 2 + to_core
+            blocks[h, m] = sums[:, :128]
+            blocks[h + 1, m] = sums[:, 128:]
+        if r + SLOTS < ROUNDS:
+            fetch(r + SLOTS).start()
+
+    def write_ids():
+        for copy in small:
+            copy.wait()
+        levels = ids[...].astype(jnp.float32).reshape(64, 16)
+        lane = lax.broadcasted_iota(jnp.int32, (16, 128), 1)
+        entry = lax.broadcasted_iota(jnp.int32, (16, 128), 0)
+        place = (lane == entry + (s % 8) * 16).astype(jnp.float32)
+        spread = jnp.dot(levels, place, preferred_element_type=jnp.float32)
+        for b in range(4):
+            for k in range(16):
+                id_rows[k // 4, b * 4 + k % 4] = spread[b * 16 + k : b * 16 + k + 1, :]
+        for h in range(4):
+            id_rows[h, 16] = (
+                anchors[here // 4, pl.ds(h * 4 + here % 4, 1), :].astype(jnp.float32) * row_scale[...]
+            )
 
     def slot_of(k):
         return jnp.where(k == 0, y, 3 + k)
@@ -138,35 +135,44 @@
     def send_ids(r, k):
         send(r, k, id_rows.at[slot_of(k), target(r)[2]], id_got.at[s], if_send, if_recv)
 
-    for k in range(1, NY):
-        pltpu.make_async_remote_copy(
-            src_ref=id_rows.at[(y + k) % NY], dst_ref=id_rows.at[3 + k],
-            send_sem=iy_send, recv_sem=iy_recv.at[k - 1],
-            device_id=(s, (y + k) % NY), device_id_type=MESH,
-        ).start()
-    for r in range(LEAD):
+    for r in range(AHEAD):
+        prefix(r)
+    pl.semaphore_wait(barrier, 66)
+    for r in range(ROUNDS):
+        if r + AHEAD < ROUNDS:
+            prefix(r + AHEAD)
         pass_on(r)
-        send_block(r, 0)
-    for r in range(LEAD, ROUNDS):
-        pass_on(r)
-    for k in range(1, NY):
-        pltpu.make_async_copy(id_rows.at[3 + k], id_rows.at[3 + k], iy_recv.at[k - 1]).wait()
-    for r in range(ROUNDS):
-        for k in range(NY):
-            send_ids(r, k)
+        if r < LEAD:
+            send_block(r, 0)
+        if r == 2:
+            for k in range(1, NY):
+                pltpu.make_async_remote_copy(
+                    src_ref=id_rows.at[(y + k) % NY], dst_ref=id_rows.at[3 + k],
+                    send_sem=iy_send, recv_sem=iy_recv.at[k - 1],
+                    device_id=(s, (y + k) % NY), device_id_type=MESH,
+                ).start()
+        if r == 1:
+            write_ids()
     own = slot_of((y - x + NX) % NX)
-    id_got[s] = id_rows[own, here]
-    anchor_out[...] = id_rows[own, 16]
     for r in range(ROUNDS):
         for i in range(NX):
             k = (y - x - i - 2 * core - (1 if ORDER[r][0] < 0 else 0) + 12) % 4
-            if r + LEAD < ROUNDS:
-                pl.when(k == 0)(functools.partial(send_block, r + LEAD, 0))
+            if r >= LEAD:
+                pl.when(k == 0)(functools.partial(send_block, r, 0))
 
             @pl.when(k != 0)
             def _():
                 pltpu.make_async_copy(blocks.at[3 + k, 0], blocks.at[3 + k, 0], y_recv.at[k - 1, r]).wait()
                 send_block(r, k)
+
+        if r == IDS_AT:
+            for k in range(1, NY):
+                pltpu.make_async_copy(id_rows.at[3 + k], id_rows.at[3 + k], iy_recv.at[k - 1]).wait()
+            for n in range(ROUNDS):
+                for k in range(NY):
+                    send_ids(n, k)
+            id_got[s] = id_rows[own, here]
+            anchor_out[...] = id_rows[own, 16]
 
     pltpu.make_async_copy(id_got.at[pl.ds(0, 63)], id_got.at[pl.ds(0, 63)], if_recv).wait()
     entry = lax.broadcasted_iota(jnp.int32, (16, 128), 0).astype(jnp.float32)
@@ -285,7 +291,7 @@
 
 def on_device(delta_codes, scale_index, anchor_codes, scale_table, anchor_scale):
     grown, totals, anchor = exchange(
-        delta_codes, scale_index, anchor_codes, anchor_scale.reshape(1, 128), scale_table
+        delta_codes.reshape(4, 4, 4, 256, 128), scale_index, anchor_codes, anchor_scale.reshape(1, 128), scale_table
     )
     return finish(grown, totals, anchor).reshape(1, 1, 16384, 128)
 

time: 111 us -> 109 us (0.982)
    pallas_call x1, Pallas kernels: 107 us -> 105 us  [exchange(): pl.pallas_call(exchange_kernel, out_shape=(jax.ShapeDtypeStruct((64, 256,...]
where the time goes in v3:
time: 109 us; the launch traced here: 108 us
  Pallas kernels  108 us (99%)
    pallas_call x1, Pallas kernels, exchange(): pl.pallas_call(exchange_kernel, out_shape=(jax.ShapeDtypeStruct((64, 256,...  105 us

profile of v3, /device:TPU:3, one launch (start us, length us, event | category | flops | bytes accessed | tf_op | source)
XLA Modules:
  0.0 107.6 jit_solution(16263395905458607393)
XLA Ops:
  0.0 105.4 %exchange.1 = (f32[64,256,128]{2,1,0:T(8,128)S(1)}, f32[64,128]{1,0:T(8,128)S(1)}, f32[1,128]{1,0:T(1,128)S(1)}) custom-call(s32[4,4,4,256,128]{4,3,2,1,0:T(8,128)} %bitcast.3, s32[4,16,16]{2,1,0:T(8,128)} %ids_hbm.1, s32[4,16,128]{2,1,0:T(8,128)} %anchors_hbm.1, f32[1,128]{1,0:T(1,128)} %bitcast.4, f32[16,128]{1,0:T(8,128)} %table_hbm.1), custom_call_target="tpu_custom_call" | custom-call | tf_op jit(solution)/shard_map/exchange/pallas_call | solution.py:217
  105.4 2.2 %finish.1 = bf16[64,256,128]{2,1,0:T(8,128)(2,1)} custom-call(f32[64,256,128]{2,1,0:T(8,128)S(1)} %get-tuple-element.8.grown, f32[64,128]{1,0:T(8,128)S(1)} %get-tuple-element.9.totals, f32[1,128]{1,0:T(1,128)S(1)} %get-tuple-element.10.anchor), custom_call_target="tpu_custom_call" | custom-call | tf_op jit(solution)/shard_map/finish/pallas_call | solution.py:278

commit v4 on v3

--- a/solution.py
+++ b/solution.py
@@ -48,7 +48,19 @@
             codes.at[m // 4, :, m % 4], stage.at[r % SLOTS], stage_sem.at[r % SLOTS]
         )
 
-    for r in range(SLOTS):
+    for r in range(AHEAD):
+        fetch(r).start()
+    barrier = pltpu.get_barrier_semaphore()
+
+    def greet(j, _):
+        pl.semaphore_signal(barrier, inc=1, device_id=((s + j) % 64, y), device_id_type=MESH)
+        return 0
+
+    lax.fori_loop(24, 64, greet, 0)
+    lax.fori_loop(1, 24, greet, 0)
+    for k in range(1, NY):
+        pl.semaphore_signal(barrier, inc=1, device_id=(s, (y + k) % NY), device_id_type=MESH)
+    for r in range(AHEAD, SLOTS):
         fetch(r).start()
     small = [
         pltpu.make_async_copy(ids_hbm, ids, small_sem.at[0]),
@@ -58,16 +70,6 @@
     ]
     for copy in small:
         copy.start()
-
-    barrier = pltpu.get_barrier_semaphore()
-
-    def greet(j, _):
-        pl.semaphore_signal(barrier, inc=1, device_id=((s + j) % 64, y), device_id_type=MESH)
-        return 0
-
-    for k in range(1, NY):
-        pl.semaphore_signal(barrier, inc=1, device_id=(s, (y + k) % NY), device_id_type=MESH)
-    lax.fori_loop(1, 64, greet, 0)
 
     row = lax.broadcasted_iota(jnp.int32, (256, 256), 0)
     col = lax.broadcasted_iota(jnp.int32, (256, 256), 1)
@@ -156,7 +158,7 @@
     own = slot_of((y - x + NX) % NX)
     for r in range(ROUNDS):
         for i in range(NX):
-            k = (y - x - i - 2 * core - (1 if ORDER[r][0] < 0 else 0) + 12) % 4
+            k = (y - x - i - core - (2 if ORDER[r][0] < 0 else 0) + 12) % 4
             if r >= LEAD:
                 pl.when(k == 0)(functools.partial(send_block, r, 0))
 

time: 109 us -> 109 us (level)
  no operation moved by 1% of the time
where the time goes in v4:
time: 109 us; the launch traced here: 108 us
  Pallas kernels  108 us (99%)
    pallas_call x1, Pallas kernels, exchange(): pl.pallas_call(exchange_kernel, out_shape=(jax.ShapeDtypeStruct((64, 256,...  105 us

profile of v4, /device:TPU:3, one launch (start us, length us, event | category | flops | bytes accessed | tf_op | source)
XLA Modules:
  0.0 107.6 jit_solution(10280012672262191285)
XLA Ops:
  0.0 105.4 %exchange.1 = (f32[64,256,128]{2,1,0:T(8,128)S(1)}, f32[64,128]{1,0:T(8,128)S(1)}, f32[1,128]{1,0:T(1,128)S(1)}) custom-call(s32[4,4,4,256,128]{4,3,2,1,0:T(8,128)} %bitcast.3, s32[4,16,16]{2,1,0:T(8,128)} %ids_hbm.1, s32[4,16,128]{2,1,0:T(8,128)} %anchors_hbm.1, f32[1,128]{1,0:T(1,128)} %bitcast.4, f32[16,128]{1,0:T(8,128)} %table_hbm.1), custom_call_target="tpu_custom_call" | custom-call | tf_op jit(solution)/shard_map/exchange/pallas_call | solution.py:219
  105.4 2.2 %finish.1 = bf16[64,256,128]{2,1,0:T(8,128)(2,1)} custom-call(f32[64,256,128]{2,1,0:T(8,128)S(1)} %get-tuple-element.8.grown, f32[64,128]{1,0:T(8,128)S(1)} %get-tuple-element.9.totals, f32[1,128]{1,0:T(1,128)S(1)} %get-tuple-element.10.anchor), custom_call_target="tpu_custom_call" | custom-call | tf_op jit(solution)/shard_map/finish/pallas_call | solution.py:280
